TPU v7x, 256 devices: a whole 4x4x8 slice. The times are simulated.
256 devices in a mesh: expert: 128 (over x_hi, y, z, core), tensor: 2 (over x_lo).
Axes of the slice: x: 4 (x_hi: 2, x_lo: 2; x = x_hi * 2 + x_lo), y: 4, z: 8, core: 2. Of those that a mesh axis runs over, the one named last changes fastest.
Arguments:
- tokens: bfloat16 [65536, 768], P(('expert', 'tensor')), may hold values from -6 to 6
- norm_gain: float32 [768], replicated, may hold values from 0.25 to 1.75
- gates: float32 [65536], P(('expert', 'tensor')), may hold values from 0.25 to 1
- expert_ids: int32 [65536], P(('expert', 'tensor')), may hold values from 0 to 255, as said below
- slots: int32 [65536], P(('expert', 'tensor')), may hold values from -1 to 1, as said below
- w_in: bfloat16 [256, 768, 3072], P(('expert', 'tensor')), may hold values from -0.21875 to 0.21875
- w_out: bfloat16 [256, 768, 3072], P(('expert', 'tensor')), may hold values from -0.109375 to 0.109375
Outputs:
- mixed: bfloat16 [65536, 768], P(('expert', 'tensor'))
Inputs may be any that keep to these rules, and one draw needn't show every extreme that they name: `expert_ids`: each token's expert, 0 to 255; in every block of 256 tokens one expert, the same in all blocks, is chosen by 2 + 1 or more tokens at positions that differ from block to block. `slots`: the slot of a token is the number of earlier tokens of its block of 256 that chose the same expert, if that is below 2, else -1; so at most 2 tokens of one block reach one expert, and one expert receives exactly 2 from every block.
All inputs are finite; a program needn't handle non-finite values.
Results may differ from a plain program's by a relative error of at most 0.0037.
Values may be sent and summed in bfloat16 or wider, within the bound.
A program may use at most 64 MiB of HBM per device.

v0:
```python
import jax
import jax.numpy as jnp
from jax import lax
from jax.sharding import PartitionSpec as P


def cut_along(array, dim, size):
    lengths = array.shape
    blocks = array.reshape(*lengths[:dim], size, lengths[dim] // size, *lengths[dim + 1 :])
    return jnp.moveaxis(blocks, dim, 0)


def in_order(blocks, dim):
    blocks = jnp.moveaxis(blocks, 0, dim)
    lengths = blocks.shape
    return blocks.reshape(*lengths[:dim], lengths[dim] * lengths[dim + 1], *lengths[dim + 2 :])


def joined_exchange(array, axis, axes, splits, concats):
    sizes = [lax.axis_size(a) for a in axes]
    blocks = cut_along(array, splits[0], sizes[0])
    blocks = jnp.moveaxis(cut_along(blocks, splits[1] + 1, sizes[1]), 0, 1)
    inside = blocks.shape[2:]
    blocks = blocks.reshape(-1, *inside)
    blocks = lax.all_to_all(blocks, axis, split_axis=0, concat_axis=0, tiled=True)
    blocks = in_order(blocks.reshape(*sizes, *inside), concats[0] + 1)
    return in_order(blocks, concats[1])


def slot_mask(expert_ids, slots, experts, capacity):
    index = expert_ids * capacity + slots
    columns = jnp.arange(experts * capacity, dtype=jnp.int32)
    valid = slots >= 0
    return ((index[:, None] == columns[None, :]) & valid[:, None]).astype(jnp.bfloat16)


def normalize(tokens, norm_gain):
    values = tokens.astype(jnp.float32)
    square = jnp.mean(values * values, axis=-1, keepdims=True)
    return (values * lax.rsqrt(square + 1e-06) * norm_gain[None, :]).astype(jnp.bfloat16)


def local(tokens, norm_gain, gates, expert_ids, slots, w_in, w_out):
    tok_dev, width = tokens.shape
    n_expert = lax.axis_size("expert")
    n_tensor = lax.axis_size("tensor")
    experts = n_expert * n_tensor
    capacity = max(2, 2 * tok_dev // experts)
    normed = normalize(tokens, norm_gain)
    masked = slot_mask(expert_ids, slots, experts, capacity)
    buffer = jnp.dot(masked.T, normed, preferred_element_type=jnp.float32).astype(jnp.bfloat16)
    sent = buffer.reshape(n_expert, n_tensor, capacity, width)
    arrived = joined_exchange(sent, ("expert", "tensor"), ("expert", "tensor"), (0, 1), (0, 1))
    rows = arrived.reshape(experts * capacity, width)
    hidden = jnp.maximum(jnp.dot(rows, w_in[0], preferred_element_type=jnp.float32), 0.0).astype(
        jnp.bfloat16
    )
    result = lax.dot_general(
        hidden, w_out[0], (((1,), (1,)), ((), ())), preferred_element_type=jnp.float32
    )
    result = result.astype(jnp.bfloat16).reshape(n_expert, n_tensor, capacity, width)
    returned = joined_exchange(result, ("expert", "tensor"), ("expert", "tensor"), (0, 1), (0, 1))
    picked = jnp.dot(
        masked, returned.reshape(experts * capacity, width), preferred_element_type=jnp.float32
    )
    return (tokens.astype(jnp.float32) + gates[:, None] * picked).astype(jnp.bfloat16)


def solution(mesh):
    in_specs = (
        P(("expert", "tensor"), None),
        P(),
        P(("expert", "tensor")),
        P(("expert", "tensor")),
        P(("expert", "tensor")),
        P(("expert", "tensor"), None, None),
        P(("expert", "tensor"), None, None),
    )
    out_specs = P(("expert", "tensor"), None)
    return jax.shard_map(local, mesh=mesh, in_specs=in_specs, out_specs=out_specs, check_vma=False)
```

profile of v0, /device:TPU:1, one launch (start us, length us, event | category | flops | bytes accessed | tf_op | source)
XLA Modules:
  0.0 89.0 jit_solution(15588611518067541169)
XLA Ops:
  0.0 0.7 broadcast_compare_fusion
  0.7 0.7 multiply_add_fusion
  1.4 1.2 %fusion.8 = f32[256]{0:T(256)S(1)} fusion(bf16[256,768]{1,0:T(8,128)(2,1)} %param.7), kind=kLoop, calls=%fused_computation.11 | loop fusion | flops 589568 | bytes 394240 | tf_op jit(solution)/shard_map/reduce_sum | solution.py:39
  2.5 1.6 %convolution_convert_fusion = bf16[512,768]{1,0:T(8,128)(2,1)S(1)} fusion(bf16[256,768]{1,0:T(8,128)(2,1)} %param.7, f32[768]{0:T(1024)} %param.8, f32[256]{0:T(256)S(1)} %add_rsqrt_fusion, s32[256]{0:T(256)S(1)} %multiply_add_fusion, pred[256]{0:T(512)(128)(4,1)S(1)} %broadcast_compare_fusion), kind=kOutput, calls=%fused_computation.5 | convolution fusion | flops 202768384 | bytes 1185024 | tf_op jit(solution)/shard_map/dot_general | solution.py:51
  4.2 0.3 reshape_transpose_transpose_reshape_reshape_reshape.6
  4.5 40.9 %all_to_all.10 = bf16[256,1,1,2,768]{4,3,2,1,0:T(2,128)(2,1)S(1)} all-to-all(bf16[256,1,1,2,768]{4,3,2,1,0:T(2,128)(2,1)S(1)} %bitcast.31), channel_id=1, replica_groups=mesh['expert'=128,'tensor'=2] {'expert','tensor'}, dimensions={0} | all-to-all | bytes 1572864 | tf_op jit(solution)/shard_map/all_to_all | solution.py:25
  45.3 0.3 reshape_reshape.6
  45.6 5.2 %maximum_convert_fusion = bf16[512,3072]{1,0:T(8,128)(2,1)S(1)} fusion(bf16[512,768]{1,0:T(8,128)(2,1)S(1)} %reshape_reshape.6, bf16[1,768,3072]{2,1,0:T(8,128)(2,1)} %param.12), kind=kOutput, calls=%fused_computation | convolution fusion | flops 2419064832 | bytes 8650752 | tf_op jit(solution)/shard_map/dot_general | solution.py:55
  50.9 5.0 %fusion.3 = bf16[512,768]{1,0:T(8,128)(2,1)S(1)} fusion(bf16[512,3072]{1,0:T(8,128)(2,1)S(1)} %maximum_convert_fusion, bf16[1,768,3072]{2,1,0:T(8,128)(2,1)} %param.13), kind=kOutput, calls=%fused_computation.4 | convolution fusion | flops 2416312320 | bytes 8650752 | tf_op jit(solution)/shard_map/dot_general | solution.py:58
  55.9 0.0 copy-start
  55.9 0.0 copy-start.1
  55.9 0.3 reshape_transpose_transpose_reshape_reshape_reshape.7
  56.2 31.3 %all_to_all.11 = bf16[256,1,1,2,768]{4,3,2,1,0:T(2,128)(2,1)S(1)} all-to-all(bf16[256,1,1,2,768]{4,3,2,1,0:T(2,128)(2,1)S(1)} %bitcast.33), channel_id=1, replica_groups=mesh['expert'=128,'tensor'=2] {'expert','tensor'}, dimensions={0} | all-to-all | bytes 1572864 | tf_op jit(solution)/shard_map/all_to_all | solution.py:25
  87.5 0.3 reshape_reshape.7
  87.8 0.0 copy-done
  87.8 0.0 copy-done.1
  87.8 1.2 %fusion.7 = bf16[256,768]{1,0:T(8,128)(2,1)} fusion(bf16[512,768]{1,0:T(8,128)(2,1)S(1)} %reshape_reshape.7, bf16[256,768]{1,0:T(8,128)(2,1)S(1)} %copy-done, f32[256]{0:T(256)S(1)} %copy-done.1, s32[256]{0:T(256)S(1)} %multiply_add_fusion, pred[256]{0:T(512)(128)(4,1)S(1)} %broadcast_compare_fusion), kind=kOutput, calls=%fused_computation.8 | convolution fusion | flops 202375168 | bytes 1575168 | tf_op jit(solution)/shard_map/dot_general | solution.py:63
  (1 shorter events, 0.0 us)
Async XLA Ops:
  55.9 31.9 %copy-start = (bf16[256,768]{1,0:T(8,128)(2,1)S(1)}, bf16[256,768]{1,0:T(8,128)(2,1)}, u32[]{:S(2)}) copy-start(bf16[256,768]{1,0:T(8,128)(2,1)} %param.7) | copy-start | bytes 1179652
  55.9 31.9 %copy-start.1 = (f32[256]{0:T(256)S(1)}, f32[256]{0:T(256)}, u32[]{:S(2)}) copy-start(f32[256]{0:T(256)} %param.9) | copy-start | bytes 3076
where the time goes:
time: 89.3 us; the launch traced here: 89 us
  blocking collectives  72.2 us (81%)
  matrix products  13 us (15%)
  other arithmetic  2.54 us (3%)
  local copies, waits for them, and re-layouts  1.2 us (1%)
    all_to_all x2, blocking collectives, joined_exchange(): lax.all_to_all(blocks, axis, split_axis=0, concat_axis=0, tiled=True)  72.2 us
    dot_general x1, matrix products, local(): jnp.dot(rows, w_in[0], preferred_element_type=jnp.float32)  5.23 us
    dot_general x1, matrix products, local(): lax.dot_general(hidden, w_out[0], (((1,), (1,)), ((), ())), preferred_ele...  4.97 us

commit v1 on v0

v1 whole, which is shorter than its diff:
```python
import functools

import jax
import jax.numpy as jnp
from jax import lax
from jax.experimental import pallas as pl
from jax.experimental.pallas import tpu as pltpu
from jax.sharding import PartitionSpec as P

MESH = pl.DeviceIdType.MESH
NX, NY, NZ, NC = 4, 4, 8, 2
N = NX * NY * NZ * NC


def position():
    e, t = lax.axis_index("expert"), lax.axis_index("tensor")
    core, z, y, xh = lax.rem(e, NC), lax.rem(e // NC, NZ), lax.rem(e // (NC * NZ), NY), e // (NC * NZ * NY)
    return xh * 2 + t, y, z, core


def device_at(here, dx, dy, dz, dc):
    x, y, z, core = here
    x, y, z, core = lax.rem(x + dx, NX), lax.rem(y + dy, NY), lax.rem(z + dz, NZ), lax.rem(core + dc, NC)
    return ((x // 2 * NY + y) * NZ + z) * NC + core, lax.rem(x, 2)


def in_plane(i):
    return lax.rem(i, NX), i // (NX * NC), lax.rem(i // NX, NC)


def enter(here, met):
    barrier = pltpu.get_barrier_semaphore()
    plane = NX * NY * NC - 1

    def greet(i, _):
        dx, dy, dc = in_plane(i + 1)
        pl.semaphore_signal(barrier, inc=1, device_id=device_at(here, dx, dy, 0, dc), device_id_type=MESH)
        return 0

    lax.fori_loop(0, plane, greet, 0)
    for dz in range(1, NZ):
        pl.semaphore_signal(barrier, inc=1, device_id=device_at(here, 0, 0, dz, 0), device_id_type=MESH)
    pl.semaphore_wait(barrier, plane + NZ - 1)
    for dz in range(1, NZ):
        pl.semaphore_signal(met, inc=1, device_id=device_at(here, 0, 0, dz, 0), device_id_type=MESH)
    pl.semaphore_wait(met, NZ - 1)


def exchange_kernel(src, dst, met, send_sem, recv_sem):
    here = position()
    e, t = lax.axis_index("expert"), lax.axis_index("tensor")
    me = e * 2 + t
    enter(here, met)

    def send(i, _):
        i = i + 1
        dz = lax.rem(i, NZ)
        dx, dy, dc = in_plane(i // NZ)
        to = device_at(here, dx, dy, dz, dc)
        pltpu.make_async_remote_copy(
            src.at[to[0] * 2 + to[1]], dst.at[me], send_sem, recv_sem, device_id=to, device_id_type=MESH
        ).start()
        return 0

    lax.fori_loop(0, N - 1, send, 0)
    dst[me] = src[me]
    rest = pltpu.make_async_remote_copy(
        src.at[pl.ds(0, N - 1)], dst.at[pl.ds(0, N - 1)], send_sem, recv_sem,
        device_id=device_at(here, 0, 0, 0, 1), device_id_type=MESH,
    )
    rest.wait_send()
    rest.wait_recv()


def exchange(blocks):
    return pl.pallas_call(
        exchange_kernel,
        out_shape=jax.ShapeDtypeStruct(blocks.shape, blocks.dtype),
        in_specs=[pl.BlockSpec(memory_space=pltpu.VMEM)],
        out_specs=pl.BlockSpec(memory_space=pltpu.VMEM),
        scratch_shapes=[
            pltpu.SemaphoreType.REGULAR,
            pltpu.SemaphoreType.DMA,
            pltpu.SemaphoreType.DMA,
        ],
        compiler_params=pltpu.CompilerParams(collective_id=0, has_side_effects=True),
    )(blocks)


def slot_mask(expert_ids, slots, experts, capacity):
    index = expert_ids * capacity + slots
    columns = jnp.arange(experts * capacity, dtype=jnp.int32)
    valid = slots >= 0
    return ((index[:, None] == columns[None, :]) & valid[:, None]).astype(jnp.bfloat16)


def normalize(tokens, norm_gain):
    values = tokens.astype(jnp.float32)
    square = jnp.mean(values * values, axis=-1, keepdims=True)
    return (values * lax.rsqrt(square + 1e-06) * norm_gain[None, :]).astype(jnp.bfloat16)


def local(tokens, norm_gain, gates, expert_ids, slots, w_in, w_out):
    tok_dev, width = tokens.shape
    experts, capacity = N, 2
    normed = normalize(tokens, norm_gain)
    masked = slot_mask(expert_ids, slots, experts, capacity)
    buffer = jnp.dot(masked.T, normed, preferred_element_type=jnp.float32).astype(jnp.bfloat16)
    arrived = exchange(buffer.reshape(experts, capacity, width))
    rows = arrived.reshape(experts * capacity, width)
    hidden = jnp.maximum(jnp.dot(rows, w_in[0], preferred_element_type=jnp.float32), 0.0).astype(
        jnp.bfloat16
    )
    result = lax.dot_general(
        hidden, w_out[0], (((1,), (1,)), ((), ())), preferred_element_type=jnp.float32
    )
    returned = exchange(result.astype(jnp.bfloat16).reshape(experts, capacity, width))
    picked = jnp.dot(
        masked, returned.reshape(experts * capacity, width), preferred_element_type=jnp.float32
    )
    return (tokens.astype(jnp.float32) + gates[:, None] * picked).astype(jnp.bfloat16)


def solution(mesh):
    in_specs = (
        P(("expert", "tensor"), None),
        P(),
        P(("expert", "tensor")),
        P(("expert", "tensor")),
        P(("expert", "tensor")),
        P(("expert", "tensor"), None, None),
        P(("expert", "tensor"), None, None),
    )
    out_specs = P(("expert", "tensor"), None)
    return jax.shard_map(local, mesh=mesh, in_specs=in_specs, out_specs=out_specs, check_vma=False)
```

time: 89.3 us -> 89.4 us (level)
  blocking collectives: 72.2 us -> 0 us
  Pallas kernels: 0 us -> 66.5 us
  local copies, waits for them, and re-layouts: 1.2 us -> 6.9 us
    all_to_all x2 -> x0, blocking collectives: 72.2 us -> none  [joined_exchange(): lax.all_to_all(blocks, axis, split_axis=0, concat_axis=0, tiled=True)]
    pallas_call x0 -> x2, Pallas kernels: none -> 66.5 us  [exchange(): pl.pallas_call(exchange_kernel, out_shape=jax.ShapeDtypeStruct(blocks.sha...]
    reshape x0 -> x4, local copies, waits for them, and re-layouts: none -> 6.88 us  [the longest x1 2.27 us: local(): rows = arrived.reshape(experts * capacity, width)]
    another operation x4 -> x0, local copies, waits for them, and re-layouts: 1.18 us -> none  [the longest x2 0.59 us: joined_exchange(): blocks = blocks.reshape(-1, *inside)]
where the time goes in v1:
time: 89.4 us; the launch traced here: 89 us
  Pallas kernels  66.5 us (74%)
  matrix products  13 us (15%)
  local copies, waits for them, and re-layouts  6.9 us (8%)
  other arithmetic  2.54 us (3%)
    pallas_call x2, Pallas kernels, exchange(): pl.pallas_call(exchange_kernel, out_shape=jax.ShapeDtypeStruct(blocks.sha...  66.5 us
    dot_general x1, matrix products, local(): jnp.dot(rows, w_in[0], preferred_element_type=jnp.float32)  5.23 us
    dot_general x1, matrix products, local(): lax.dot_general(hidden, w_out[0], (((1,), (1,)), ((), ())), preferred_ele...  4.98 us
    reshape x1, local copies, waits for them, and re-layouts, local(): rows = arrived.reshape(experts * capacity, width)  2.27 us
    reshape x1, local copies, waits for them, and re-layouts, local(): returned.reshape(experts * capacity, width)  2.27 us

profile of v1, /device:TPU:1, one launch (start us, length us, event | category | flops | bytes accessed | tf_op | source)
XLA Modules:
  0.0 89.0 jit_solution(15442716327188303229)
XLA Ops:
  0.0 0.7 broadcast_compare_fusion
  0.7 0.7 multiply_add_fusion
  1.4 1.2 %fusion.8 = f32[256]{0:T(256)S(1)} fusion(bf16[256,768]{1,0:T(8,128)(2,1)} %param.7), kind=kLoop, calls=%fused_computation.11 | loop fusion | flops 589568 | bytes 394240 | tf_op jit(solution)/shard_map/reduce_sum | solution.py:99
  2.5 1.6 %convolution_convert_fusion = bf16[512,768]{1,0:T(8,128)(2,1)S(1)} fusion(bf16[256,768]{1,0:T(8,128)(2,1)} %param.7, f32[768]{0:T(1024)} %param.8, f32[256]{0:T(256)S(1)} %add_rsqrt_fusion, s32[256]{0:T(256)S(1)} %multiply_add_fusion, pred[256]{0:T(512)(128)(4,1)S(1)} %broadcast_compare_fusion), kind=kOutput, calls=%fused_computation.5 | convolution fusion | flops 202768384 | bytes 1185024 | tf_op jit(solution)/shard_map/dot_general | solution.py:108
  4.2 1.2 %reshape.24.src = bf16[256,2,768]{2,1,0:T(2,128)(2,1)} reshape(bf16[512,768]{1,0:T(8,128)(2,1)S(1)} %convolution_convert_fusion) | data formatting | bytes 1572864 | tf_op jit(solution)/shard_map/reshape | solution.py:109
  5.3 36.4 %shard_map.73 = bf16[256,2,768]{2,1,0:T(2,128)(2,1)} custom-call(bf16[256,2,768]{2,1,0:T(2,128)(2,1)} %reshape.24.src), custom_call_target="tpu_custom_call" | custom-call | tf_op jit(solution)/shard_map/pallas_call | solution.py:76
  41.8 2.3 %reshape.25 = bf16[512,768]{1,0:T(8,128)(2,1)S(1)} reshape(bf16[256,2,768]{2,1,0:T(2,128)(2,1)} %shard_map.73) | data formatting | bytes 1572864 | tf_op jit(solution)/shard_map/reshape | solution.py:110
  44.0 5.2 %maximum_convert_fusion = bf16[512,3072]{1,0:T(8,128)(2,1)S(1)} fusion(bf16[512,768]{1,0:T(8,128)(2,1)S(1)} %reshape.25, bf16[1,768,3072]{2,1,0:T(8,128)(2,1)} %param.12), kind=kOutput, calls=%fused_computation | convolution fusion | flops 2419064832 | bytes 8650752 | tf_op jit(solution)/shard_map/dot_general | solution.py:111
  49.3 5.0 %fusion.3 = bf16[512,768]{1,0:T(8,128)(2,1)S(1)} fusion(bf16[512,3072]{1,0:T(8,128)(2,1)S(1)} %maximum_convert_fusion, bf16[1,768,3072]{2,1,0:T(8,128)(2,1)} %param.13), kind=kOutput, calls=%fused_computation.4 | convolution fusion | flops 2416312320 | bytes 8650752 | tf_op jit(solution)/shard_map/dot_general | solution.py:114
  54.3 0.0 copy-start
  54.3 0.0 copy-start.1
  54.3 1.2 %reshape.26.src = bf16[256,2,768]{2,1,0:T(2,128)(2,1)} reshape(bf16[512,768]{1,0:T(8,128)(2,1)S(1)} %fusion.3) | data formatting | bytes 1572864 | tf_op jit(solution)/shard_map/reshape | solution.py:117
  55.4 30.1 %shard_map.74 = bf16[256,2,768]{2,1,0:T(2,128)(2,1)} custom-call(bf16[256,2,768]{2,1,0:T(2,128)(2,1)} %reshape.26.src), custom_call_target="tpu_custom_call" | custom-call | tf_op jit(solution)/shard_map/pallas_call | solution.py:76
  85.6 2.3 %reshape.27 = bf16[512,768]{1,0:T(8,128)(2,1)S(1)} reshape(bf16[256,2,768]{2,1,0:T(2,128)(2,1)} %shard_map.74) | data formatting | bytes 1572864 | tf_op jit(solution)/shard_map/reshape | solution.py:119
  87.8 0.0 copy-done
  87.8 0.0 copy-done.1
  87.9 1.2 %fusion.7 = bf16[256,768]{1,0:T(8,128)(2,1)} fusion(bf16[512,768]{1,0:T(8,128)(2,1)S(1)} %reshape.27, bf16[256,768]{1,0:T(8,128)(2,1)S(1)} %copy-done, f32[256]{0:T(256)S(1)} %copy-done.1, s32[256]{0:T(256)S(1)} %multiply_add_fusion, pred[256]{0:T(512)(128)(4,1)S(1)} %broadcast_compare_fusion), kind=kOutput, calls=%fused_computation.8 | convolution fusion | flops 202375168 | bytes 1575168 | tf_op jit(solution)/shard_map/dot_general | solution.py:118
  (1 shorter events, 0.0 us)
Async XLA Ops:
  54.3 33.6 %copy-start = (bf16[256,768]{1,0:T(8,128)(2,1)S(1)}, bf16[256,768]{1,0:T(8,128)(2,1)}, u32[]{:S(2)}) copy-start(bf16[256,768]{1,0:T(8,128)(2,1)} %param.7) | copy-start | bytes 1179652
  54.3 33.6 %copy-start.1 = (f32[256]{0:T(256)S(1)}, f32[256]{0:T(256)}, u32[]{:S(2)}) copy-start(f32[256]{0:T(256)} %param.9) | copy-start | bytes 3076

commit v2 on v1

v2 whole, which is shorter than its diff:
```python
import functools

import jax
import jax.numpy as jnp
from jax import lax
from jax.experimental import pallas as pl
from jax.experimental.pallas import tpu as pltpu
from jax.sharding import PartitionSpec as P

MESH = pl.DeviceIdType.MESH
NX, NY, NZ, NC = 4, 4, 8, 2
N = NX * NY * NZ * NC
LANES, ROWS = 128, 16
CHUNKS = ((0, 2), (1, 2))
PARTNERS = N // len(CHUNKS)
ALONG_Z = NZ // len(CHUNKS)
TILES = PARTNERS * 2 // ROWS


def position():
    e, t = lax.axis_index("expert"), lax.axis_index("tensor")
    core, z, y, xh = lax.rem(e, NC), lax.rem(e // NC, NZ), lax.rem(e // (NC * NZ), NY), e // (NC * NZ * NY)
    return xh * 2 + t, y, z, core


def device_at(here, dx, dy, dz, dc):
    x, y, z, core = here
    x, y, z, core = lax.rem(x + dx, NX), lax.rem(y + dy, NY), lax.rem(z + dz, NZ), lax.rem(core + dc, NC)
    return ((x // 2 * NY + y) * NZ + z) * NC + core, lax.rem(x, 2)


def in_plane(i):
    return lax.rem(i, NX), i // (NX * NC), lax.rem(i // NX, NC)


def partner(here, chunk, i, sign):
    first, step = CHUNKS[chunk]
    dz = lax.rem(first + step * lax.rem(i, ALONG_Z), NZ)
    dx, dy, dc = in_plane(i // ALONG_Z)
    if sign < 0:
        dx, dy, dz = NX - dx, NY - dy, NZ - dz
    return device_at(here, dx, dy, dz, dc)


def pair(ref, i):
    return ref.at[i // 8, :, pl.ds(2 * lax.rem(i, 8), 2), :]


def greet(here):
    barrier = pltpu.get_barrier_semaphore()

    def signal(i, _):
        dx, dy, dc = in_plane(i + 1)
        pl.semaphore_signal(barrier, inc=1, device_id=device_at(here, dx, dy, 0, dc), device_id_type=MESH)
        return 0

    lax.fori_loop(0, NX * NY * NC - 1, signal, 0)
    for dz in range(1, NZ):
        pl.semaphore_signal(barrier, inc=1, device_id=device_at(here, 0, 0, dz, 0), device_id_type=MESH)


def meet(here, met):
    pl.semaphore_wait(pltpu.get_barrier_semaphore(), NX * NY * NC + NZ - 2)
    for dz in range(1, NZ):
        pl.semaphore_signal(met, inc=1, device_id=device_at(here, 0, 0, dz, 0), device_id_type=MESH)
    pl.semaphore_wait(met, NZ - 1)


def columns(ref, tiles, count):
    return jnp.concatenate([ref[tiles, j].reshape(count * ROWS, LANES) for j in range(ref.shape[1])], axis=1)


def kernel(tokens, gain, gates, ids, slots, w_in, w_out, mixed,
           outbox, inbox, results, returned, w1, w2, hidden,
           met, w_sem, out_sem, in_sem, back_sem, home_sem):
    here = position()
    me = lax.axis_index("expert") * 2 + lax.axis_index("tensor")
    n_tok, width = tokens.shape
    parts = width // LANES
    load1 = pltpu.make_async_copy(w_in.at[0], w1, w_sem.at[0])
    load2 = pltpu.make_async_copy(w_out.at[0], w2, w_sem.at[1])
    greet(here)
    load1.start()
    load2.start()

    values = tokens[...].astype(jnp.float32)
    square = jnp.mean(values * values, axis=-1, keepdims=True)
    normed = (values * lax.rsqrt(square + 1e-06) * gain[...]).astype(jnp.bfloat16)
    index = jnp.where(slots[...] >= 0, ids[...] * 2 + slots[...], -1)
    picks = (lax.broadcasted_iota(jnp.int32, (2 * N, n_tok), 0) == index).astype(jnp.bfloat16)
    for j in range(parts // 2):
        block = jnp.dot(picks, normed[:, j * 256 : j * 256 + 256], preferred_element_type=jnp.float32).astype(jnp.bfloat16)
        for half in range(2):
            outbox[:, 2 * j + half] = block[:, half * LANES : (half + 1) * LANES].reshape(2 * N // ROWS, ROWS, LANES)
    meet(here, met)

    def post(chunk, first):
        def send(i, _):
            to = partner(here, chunk, i, 1)
            pltpu.make_async_remote_copy(
                pair(outbox, to[0] * 2 + to[1]), pair(inbox, chunk * PARTNERS + i), out_sem, in_sem.at[chunk],
                device_id=to, device_id_type=MESH,
            ).start()
            return 0

        lax.fori_loop(first, PARTNERS, send, 0)

    post(0, 1)
    own = pltpu.make_async_copy(pair(outbox, me), pair(inbox, 0), in_sem.at[0])
    own.start()
    for chunk in range(1, len(CHUNKS)):
        post(chunk, 0)
    load1.wait()
    load2.wait()

    near = device_at(here, 0, 0, 0, 1)
    for chunk in range(len(CHUNKS)):
        tiles = pl.ds(chunk * TILES, TILES)
        pltpu.make_async_remote_copy(
            inbox.at[tiles], inbox.at[tiles], out_sem, in_sem.at[chunk], device_id=near, device_id_type=MESH
        ).wait_recv()
        rows = columns(inbox, tiles, TILES)

        def widen(k, _):
            at = pl.ds(pl.multiple_of(k * 256, 256), 256)
            h = jnp.dot(rows, w1[:, at], preferred_element_type=jnp.float32)
            hidden[:, at] = jnp.maximum(h, 0.0).astype(jnp.bfloat16)
            return 0

        lax.fori_loop(0, w1.shape[1] // 256, widen, 0)
        for j in range(parts // 2):
            r = lax.dot_general(
                hidden[...], w2[j * 256 : j * 256 + 256, :], (((1,), (1,)), ((), ())), preferred_element_type=jnp.float32
            ).astype(jnp.bfloat16)
            for half in range(2):
                results[tiles, 2 * j + half] = r[:, half * LANES : (half + 1) * LANES].reshape(TILES, ROWS, LANES)

        def reply(i, _):
            to = partner(here, chunk, i, -1)
            pltpu.make_async_remote_copy(
                pair(results, chunk * PARTNERS + i), pair(returned, me), back_sem, home_sem,
                device_id=to, device_id_type=MESH,
            ).start()
            return 0

        lax.fori_loop(1 if chunk == 0 else 0, PARTNERS, reply, 0)
        if chunk == 0:
            pltpu.make_async_copy(pair(results, 0), pair(returned, me), home_sem).start()

    everything = pltpu.make_async_remote_copy(returned, returned, back_sem, home_sem, device_id=near, device_id_type=MESH)
    everything.wait_recv()
    rest = columns(returned, slice(None), 2 * N // ROWS)
    picked = lax.dot_general(picks, rest, (((0,), (0,)), ((), ())), preferred_element_type=jnp.float32)
    weight = jnp.transpose(jnp.broadcast_to(gates[...], (LANES, n_tok)))
    weight = jnp.concatenate([weight] * parts, axis=1)
    mixed[...] = (tokens[...].astype(jnp.float32) + weight * picked).astype(jnp.bfloat16)
    left = 2 * N // ROWS - 1
    for box, sem in ((outbox, out_sem), (results, back_sem)):
        pltpu.make_async_copy(box.at[pl.ds(0, left)], box.at[pl.ds(0, left)], sem).wait()
        pltpu.make_async_copy(box.at[0, :, pl.ds(0, ROWS - 2), :], box.at[0, :, pl.ds(0, ROWS - 2), :], sem).wait()


def local(tokens, norm_gain, gates, expert_ids, slots, w_in, w_out):
    n_tok, width = tokens.shape
    hidden = w_in.shape[2]
    box = pltpu.VMEM((2 * N // ROWS, width // LANES, ROWS, LANES), jnp.bfloat16)
    vmem, anywhere = pl.BlockSpec(memory_space=pltpu.VMEM), pl.BlockSpec(memory_space=pl.ANY)
    return pl.pallas_call(
        kernel,
        out_shape=jax.ShapeDtypeStruct(tokens.shape, tokens.dtype),
        in_specs=[vmem] * 5 + [anywhere] * 2,
        out_specs=vmem,
        scratch_shapes=[
            box, box, box, box,
            pltpu.VMEM((width, hidden), jnp.bfloat16),
            pltpu.VMEM((width, hidden), jnp.bfloat16),
            pltpu.VMEM((PARTNERS * 2, hidden), jnp.bfloat16),
            pltpu.SemaphoreType.REGULAR,
            pltpu.SemaphoreType.DMA((2,)),
            pltpu.SemaphoreType.DMA,
            pltpu.SemaphoreType.DMA((len(CHUNKS),)),
            pltpu.SemaphoreType.DMA,
            pltpu.SemaphoreType.DMA,
        ],
        compiler_params=pltpu.CompilerParams(collective_id=0, has_side_effects=True),
    )(tokens, norm_gain.reshape(1, width), gates.reshape(1, n_tok), expert_ids.reshape(1, n_tok),
      slots.reshape(1, n_tok), w_in, w_out)


def solution(mesh):
    in_specs = (
        P(("expert", "tensor"), None),
        P(),
        P(("expert", "tensor")),
        P(("expert", "tensor")),
        P(("expert", "tensor")),
        P(("expert", "tensor"), None, None),
        P(("expert", "tensor"), None, None),
    )
    out_specs = P(("expert", "tensor"), None)
    return jax.shard_map(local, mesh=mesh, in_specs=in_specs, out_specs=out_specs, check_vma=False)
```

time: 89.4 us -> 63.4 us (0.71)
  matrix products: 13 us -> 0 us
  Pallas kernels: 66.5 us -> 60.2 us
  local copies, waits for them, and re-layouts: 6.9 us -> 3.03 us
  other arithmetic: 2.54 us -> 0 us
    dot_general x4 -> x0, matrix products: 13 us -> none  [the longest x1 5.23 us: local(): jnp.dot(rows, w_in[0], preferred_element_type=jnp.float32)]
    pallas_call x2 -> x1, Pallas kernels: 66.5 us -> 60.2 us  [local(): pl.pallas_call(kernel, out_shape=jax.ShapeDtypeStruct(tokens.shape, token...]
    reshape x4 -> x1, local copies, waits for them, and re-layouts: 6.88 us -> 1.27 us  [local(): norm_gain.reshape(1, width)]
    unnamed x4 -> x1, local copies, waits for them, and re-layouts: 0.01 us -> 1.77 us
    reduce_sum x1 -> x0, other arithmetic: 1.15 us -> none  [normalize(): square = jnp.mean(values * values, axis=-1, keepdims=True)]
where the time goes in v2:
time: 63.4 us; the launch traced here: 63.2 us
  Pallas kernels  60.2 us (95%)
  local copies, waits for them, and re-layouts  3.03 us (5%)
    pallas_call x1, Pallas kernels, local(): pl.pallas_call(kernel, out_shape=jax.ShapeDtypeStruct(tokens.shape, token...  60.2 us
    unnamed x1, local copies, waits for them, and re-layouts  1.77 us

profile of v2, /device:TPU:1, one launch (start us, length us, event | category | flops | bytes accessed | tf_op | source)
XLA Modules:
  0.0 63.2 jit_solution(16025208761230523766)
XLA Ops:
  0.0 1.3 %reshape.12.gain = f32[1,768]{1,0:T(1,128)} reshape(f32[768]{0:T(1024)} %param.8) | data formatting | bytes 6144 | tf_op jit(solution)/shard_map/reshape | solution.py:186
  1.3 60.2 %shard_map.73 = bf16[256,768]{1,0:T(8,128)(2,1)} custom-call(bf16[256,768]{1,0:T(8,128)(2,1)} %tokens.1, f32[1,768]{1,0:T(1,128)} %reshape.12.gain, f32[1,256]{1,0:T(1,128)} %bitcast.3, s32[1,256]{1,0:T(1,128)} %bitcast.4, s32[1,256]{1,0:T(1,128)} %bitcast.5, bf16[1,768,3072]{2,1,0:T(8,128)(2,1)} %w_in.1, bf16[1,768,3072]{2,1,0:T(8,128)(2,1)} %w_out.1), custom_call_target="tpu_custom_call" | custom-call | tf_op jit(solution)/shard_map/pallas_call | solution.py:168
  61.5 1.8 %copy.9 = bf16[256,768]{1,0:T(8,128)(2,1)} copy(bf16[256,768]{1,0:T(8,128)(2,1)} %shard_map.73) | data formatting | bytes 786432

commit v3 on v2

v3 whole, which is shorter than its diff:
```python
import functools

import jax
import jax.numpy as jnp
from jax import lax
from jax.experimental import pallas as pl
from jax.experimental.pallas import tpu as pltpu
from jax.sharding import PartitionSpec as P

LOGICAL = pl.DeviceIdType.LOGICAL
NX, NY, NZ, NC = 4, 4, 8, 2
N = NX * NY * NZ * NC
LANES, ROWS = 128, 16
CHUNKS = ((0, 2), (1, 2))
PARTNERS = N // len(CHUNKS)
ALONG_Z = NZ // len(CHUNKS)
TILES = PARTNERS * 2 // ROWS
PLANE = [(dc, dx) for dc in range(NC) for dx in range(NX)]


class Place:
    def __init__(self):
        e, t = lax.axis_index("expert"), lax.axis_index("tensor")
        core, z = lax.rem(e, NC), lax.rem(e // NC, NZ)
        y, xh = lax.rem(e // (NC * NZ), NY), e // (NC * NZ * NY)
        self.me = e * 2 + t
        self.y = y
        xs = [lax.rem(xh * 2 + t + d, NX) for d in range(NX)]
        zs = [lax.rem(z + d, NZ) for d in range(NZ)]
        cs = [lax.rem(core + d, NC) for d in range(NC)]
        self.along_x = [(x // 2 * 128 + lax.rem(x, 2), x // 2 * 16, lax.rem(x, 2)) for x in xs]
        self.along_z = [(z * 4, z // 2, lax.rem(z, 2) * 4) for z in zs]
        self.along_c = [(c * 2, c * 2) for c in cs]

    def row(self, dy):
        y = lax.rem(self.y + dy, NY)
        return y * 32, y * 4

    def at(self, row, dx, dz, dc):
        x, z, c = self.along_x[dx], self.along_z[dz], self.along_c[dc]
        return row[0] + z[0] + (x[0] + c[0]), row[1] + z[1] + x[1], z[2] + (x[2] + c[1])


def pair(ref, tile, i):
    return ref.at[tile, :, pl.ds(2 * i, 2), :]


def greet(place):
    barrier = pltpu.get_barrier_semaphore()
    rows = [place.row(dy) for dy in range(NY)]
    for dz in range(1, NZ):
        pl.semaphore_signal(barrier, inc=1, device_id=place.at(rows[0], 0, dz, 0)[0], device_id_type=LOGICAL)
    for dy in range(NY):
        for dc, dx in PLANE:
            if dy or dc or dx:
                pl.semaphore_signal(barrier, inc=1, device_id=place.at(rows[dy], dx, 0, dc)[0], device_id_type=LOGICAL)


def columns(ref, tiles, count):
    return jnp.concatenate([ref[tiles, j].reshape(count * ROWS, LANES) for j in range(ref.shape[1])], axis=1)


def kernel(tokens_hbm, gain_hbm, gates_hbm, ids_hbm, slots_hbm, w_in, w_out, mixed,
           tokens, gain, gates, ids, slots, outbox, inbox, results, returned, w1, w2, hidden,
           met, arg_sem, w_sem, out_sem, in_sem, back_sem, home_sem):
    loads = [
        pltpu.make_async_copy(hbm, vmem, arg_sem.at[i])
        for i, (hbm, vmem) in enumerate(
            ((tokens_hbm, tokens), (gain_hbm, gain), (gates_hbm, gates), (ids_hbm, ids), (slots_hbm, slots))
        )
    ]
    for load in loads:
        load.start()
    place = Place()
    me = place.me
    n_tok, width = tokens.shape
    parts = width // LANES
    load1 = pltpu.make_async_copy(w_in.at[0], w1, w_sem.at[0])
    load2 = pltpu.make_async_copy(w_out.at[0], w2, w_sem.at[1])
    greet(place)
    for load in loads:
        load.wait()
    load1.start()
    load2.start()

    values = tokens[...].astype(jnp.float32)
    square = jnp.mean(values * values, axis=-1, keepdims=True)
    normed = (values * lax.rsqrt(square + 1e-06) * gain[...].reshape(1, width)).astype(jnp.bfloat16)
    index = jnp.where(slots[...] >= 0, ids[...] * 2 + slots[...], -1)
    picks = (lax.broadcasted_iota(jnp.int32, (2 * N, n_tok), 0) == index).astype(jnp.bfloat16)
    for j in range(parts // 2):
        block = jnp.dot(picks, normed[:, j * 256 : j * 256 + 256], preferred_element_type=jnp.float32).astype(jnp.bfloat16)
        for half in range(2):
            outbox[:, 2 * j + half] = block[:, half * LANES : (half + 1) * LANES].reshape(2 * N // ROWS, ROWS, LANES)

    here = place.row(0)

    def post(chunk, dy, row, combos):
        first, step = CHUNKS[chunk]
        for a, dc, dx in combos:
            number, tile, i = place.at(row, dx, first + step * a, dc)
            pltpu.make_async_remote_copy(
                pair(outbox, tile, i), pair(inbox, chunk * TILES + dy * ALONG_Z + a, dc * NX + dx),
                out_sem, in_sem.at[chunk], device_id=number, device_id_type=LOGICAL,
            ).start()

    pl.semaphore_wait(pltpu.get_barrier_semaphore(), NX * NY * NC + NZ - 2)
    for dz in range(1, NZ):
        pl.semaphore_signal(met, inc=1, device_id=place.at(here, 0, dz, 0)[0], device_id_type=LOGICAL)
    for chunk in range(len(CHUNKS)):
        post(chunk, 0, here, [(a, 0, 0) for a in range(1 if chunk == 0 else 0, ALONG_Z)])
    post(0, 0, here, [(0, dc, dx) for dc, dx in PLANE if dc or dx])

    def post_row(dy, _):
        post(0, dy, place.row(dy), [(0, dc, dx) for dc, dx in PLANE])
        return 0

    lax.fori_loop(1, NY, post_row, 0)
    own = pltpu.make_async_copy(pair(outbox, me // 8, lax.rem(me, 8)), pair(inbox, 0, 0), in_sem.at[0])
    own.start()
    pl.semaphore_wait(met, NZ - 1)
    for chunk in range(len(CHUNKS)):
        steps = range(1 if chunk == 0 else 0, ALONG_Z)
        post(chunk, 0, here, [(a, dc, dx) for dc, dx in PLANE for a in steps if dc or dx])

        def post_rest(dy, _):
            post(chunk, dy, place.row(dy), [(a, dc, dx) for dc, dx in PLANE for a in steps])
            return 0

        lax.fori_loop(1, NY, post_rest, 0)
    load1.wait()
    load2.wait()

    near = place.at(here, 0, 0, 1)[0]
    for chunk in range(len(CHUNKS)):
        tiles = pl.ds(chunk * TILES, TILES)
        pltpu.make_async_remote_copy(
            inbox.at[tiles], inbox.at[tiles], out_sem, in_sem.at[chunk], device_id=near, device_id_type=LOGICAL
        ).wait_recv()
        rows = columns(inbox, tiles, TILES)

        def widen(k, _):
            at = pl.ds(pl.multiple_of(k * 256, 256), 256)
            h = jnp.dot(rows, w1[:, at], preferred_element_type=jnp.float32)
            hidden[:, at] = jnp.maximum(h, 0.0).astype(jnp.bfloat16)
            return 0

        lax.fori_loop(0, w1.shape[1] // 256, widen, 0)
        for j in range(parts // 2):
            r = lax.dot_general(
                hidden[...], w2[j * 256 : j * 256 + 256, :], (((1,), (1,)), ((), ())), preferred_element_type=jnp.float32
            ).astype(jnp.bfloat16)
            for half in range(2):
                results[tiles, 2 * j + half] = r[:, half * LANES : (half + 1) * LANES].reshape(TILES, ROWS, LANES)

        home = pair(returned, me // 8, lax.rem(me, 8))

        def reply(dy, row, combos):
            first, step = CHUNKS[chunk]
            for a, dc, dx in combos:
                number = place.at(row, -dx % NX, -(first + step * a) % NZ, dc)[0]
                pltpu.make_async_remote_copy(
                    pair(results, chunk * TILES + dy * ALONG_Z + a, dc * NX + dx), home,
                    back_sem, home_sem, device_id=number, device_id_type=LOGICAL,
                ).start()

        def reply_row(dy, _):
            reply(dy, place.row(NY - dy), [(a, dc, dx) for dc, dx in PLANE for a in range(ALONG_Z)])
            return 0

        reply(0, here, [(a, dc, dx) for dc, dx in PLANE for a in range(ALONG_Z) if chunk or a or dc or dx])
        lax.fori_loop(1, NY, reply_row, 0)
        if chunk == 0:
            pltpu.make_async_copy(pair(results, 0, 0), home, home_sem).start()

    everything = pltpu.make_async_remote_copy(returned, returned, back_sem, home_sem, device_id=near, device_id_type=LOGICAL)
    everything.wait_recv()
    rest = columns(returned, slice(None), 2 * N // ROWS)
    picked = lax.dot_general(picks, rest, (((0,), (0,)), ((), ())), preferred_element_type=jnp.float32)
    weight = jnp.transpose(jnp.broadcast_to(gates[...], (LANES, n_tok)))
    weight = jnp.concatenate([weight] * parts, axis=1)
    mixed[...] = (tokens[...].astype(jnp.float32) + weight * picked).astype(jnp.bfloat16)
    left = 2 * N // ROWS - 1
    for box, sem in ((outbox, out_sem), (results, back_sem)):
        pltpu.make_async_copy(box.at[pl.ds(0, left)], box.at[pl.ds(0, left)], sem).wait()
        pltpu.make_async_copy(box.at[0, :, pl.ds(0, ROWS - 2), :], box.at[0, :, pl.ds(0, ROWS - 2), :], sem).wait()


def local(tokens, norm_gain, gates, expert_ids, slots, w_in, w_out):
    n_tok, width = tokens.shape
    hidden = w_in.shape[2]
    box = pltpu.VMEM((2 * N // ROWS, width // LANES, ROWS, LANES), jnp.bfloat16)
    vmem, anywhere = pl.BlockSpec(memory_space=pltpu.VMEM), pl.BlockSpec(memory_space=pl.ANY)
    return pl.pallas_call(
        kernel,
        out_shape=jax.ShapeDtypeStruct(tokens.shape, tokens.dtype),
        in_specs=[anywhere] * 7,
        out_specs=vmem,
        scratch_shapes=[
            pltpu.VMEM((n_tok, width), tokens.dtype),
            pltpu.VMEM((width,), jnp.float32),
            pltpu.VMEM((1, n_tok), jnp.float32),
            pltpu.VMEM((1, n_tok), jnp.int32),
            pltpu.VMEM((1, n_tok), jnp.int32),
            box, box, box, box,
            pltpu.VMEM((width, hidden), jnp.bfloat16),
            pltpu.VMEM((width, hidden), jnp.bfloat16),
            pltpu.VMEM((PARTNERS * 2, hidden), jnp.bfloat16),
            pltpu.SemaphoreType.REGULAR,
            pltpu.SemaphoreType.DMA((5,)),
            pltpu.SemaphoreType.DMA((2,)),
            pltpu.SemaphoreType.DMA,
            pltpu.SemaphoreType.DMA((len(CHUNKS),)),
            pltpu.SemaphoreType.DMA,
            pltpu.SemaphoreType.DMA,
        ],
        compiler_params=pltpu.CompilerParams(collective_id=0, has_side_effects=True),
    )(tokens, norm_gain, gates.reshape(1, n_tok), expert_ids.reshape(1, n_tok),
      slots.reshape(1, n_tok), w_in, w_out)


def solution(mesh):
    in_specs = (
        P(("expert", "tensor"), None),
        P(),
        P(("expert", "tensor")),
        P(("expert", "tensor")),
        P(("expert", "tensor")),
        P(("expert", "tensor"), None, None),
        P(("expert", "tensor"), None, None),
    )
    out_specs = P(("expert", "tensor"), None)
    return jax.shard_map(local, mesh=mesh, in_specs=in_specs, out_specs=out_specs, check_vma=False)
```

time: 63.4 us -> 58.5 us (0.923)
  Pallas kernels: 60.2 us -> 56.6 us
  local copies, waits for them, and re-layouts: 3.03 us -> 1.77 us
    pallas_call x1, Pallas kernels: 60.2 us -> 56.6 us  [local(): pl.pallas_call(kernel, out_shape=jax.ShapeDtypeStruct(tokens.shape, token...]
    reshape x1 -> x0, local copies, waits for them, and re-layouts: 1.27 us -> none  [local(): norm_gain.reshape(1, width)]
where the time goes in v3:
time: 58.5 us; the launch traced here: 58.4 us
  Pallas kernels  56.6 us (97%)
  local copies, waits for them, and re-layouts  1.77 us (3%)
    pallas_call x1, Pallas kernels, local(): pl.pallas_call(kernel, out_shape=jax.ShapeDtypeStruct(tokens.shape, token...  56.6 us
    unnamed x1, local copies, waits for them, and re-layouts  1.77 us

profile of v3, /device:TPU:1, one launch (start us, length us, event | category | flops | bytes accessed | tf_op | source)
XLA Modules:
  0.0 58.4 jit_solution(8379943275289349022)
XLA Ops:
  0.0 56.6 %shard_map.73 = bf16[256,768]{1,0:T(8,128)(2,1)} custom-call(bf16[256,768]{1,0:T(8,128)(2,1)} %tokens_hbm.1, f32[768]{0:T(1024)} %gain_hbm.1, f32[1,256]{1,0:T(1,128)} %bitcast.3, s32[1,256]{1,0:T(1,128)} %bitcast.4, s32[1,256]{1,0:T(1,128)} %bitcast.5, bf16[1,768,3072]{2,1,0:T(8,128)(2,1)} %w_in.1, bf16[1,768,3072]{2,1,0:T(8,128)(2,1)} %w_out.1), custom_call_target="tpu_custom_call" | custom-call | tf_op jit(solution)/shard_map/pallas_call | solution.py:194
  56.6 1.8 %copy.9 = bf16[256,768]{1,0:T(8,128)(2,1)} copy(bf16[256,768]{1,0:T(8,128)(2,1)} %shard_map.73) | data formatting | bytes 786432

commit v4 on v3

--- a/solution.py
+++ b/solution.py
@@ -11,10 +11,12 @@
 NX, NY, NZ, NC = 4, 4, 8, 2
 N = NX * NY * NZ * NC
 LANES, ROWS = 128, 16
+VMEM_LIMIT = 24 * 1024 * 1024
 CHUNKS = ((0, 2), (1, 2))
 PARTNERS = N // len(CHUNKS)
 ALONG_Z = NZ // len(CHUNKS)
 TILES = PARTNERS * 2 // ROWS
+GROUPS = ((0, (1, 3)), (0, (2,)), (1, (0, 3)), (1, (1, 2)))
 PLANE = [(dc, dx) for dc in range(NC) for dx in range(NX)]
 
 
@@ -60,7 +62,7 @@
     return jnp.concatenate([ref[tiles, j].reshape(count * ROWS, LANES) for j in range(ref.shape[1])], axis=1)
 
 
-def kernel(tokens_hbm, gain_hbm, gates_hbm, ids_hbm, slots_hbm, w_in, w_out, mixed,
+def kernel(tokens_hbm, gain_hbm, gates_hbm, ids_hbm, slots_hbm, w_in, w_out, gated,
            tokens, gain, gates, ids, slots, outbox, inbox, results, returned, w1, w2, hidden,
            met, arg_sem, w_sem, out_sem, in_sem, back_sem, home_sem):
     loads = [
@@ -106,7 +108,7 @@
 
     pl.semaphore_wait(pltpu.get_barrier_semaphore(), NX * NY * NC + NZ - 2)
     for dz in range(1, NZ):
-        pl.semaphore_signal(met, inc=1, device_id=place.at(here, 0, dz, 0)[0], device_id_type=LOGICAL)
+        pl.semaphore_signal(met.at[NZ - dz], inc=1, device_id=place.at(here, 0, dz, 0)[0], device_id_type=LOGICAL)
     for chunk in range(len(CHUNKS)):
         post(chunk, 0, here, [(a, 0, 0) for a in range(1 if chunk == 0 else 0, ALONG_Z)])
     post(0, 0, here, [(0, dc, dx) for dc, dx in PLANE if dc or dx])
@@ -118,13 +120,14 @@
     lax.fori_loop(1, NY, post_row, 0)
     own = pltpu.make_async_copy(pair(outbox, me // 8, lax.rem(me, 8)), pair(inbox, 0, 0), in_sem.at[0])
     own.start()
-    pl.semaphore_wait(met, NZ - 1)
-    for chunk in range(len(CHUNKS)):
-        steps = range(1 if chunk == 0 else 0, ALONG_Z)
-        post(chunk, 0, here, [(a, dc, dx) for dc, dx in PLANE for a in steps if dc or dx])
+    for chunk, group in GROUPS:
+        first, step = CHUNKS[chunk]
+        for a in group:
+            pl.semaphore_wait(met.at[first + step * a], 1)
+        post(chunk, 0, here, [(a, dc, dx) for dc, dx in PLANE for a in group if dc or dx])
 
         def post_rest(dy, _):
-            post(chunk, dy, place.row(dy), [(a, dc, dx) for dc, dx in PLANE for a in steps])
+            post(chunk, dy, place.row(dy), [(a, dc, dx) for dc, dx in PLANE for a in group])
             return 0
 
         lax.fori_loop(1, NY, post_rest, 0)
@@ -179,7 +182,7 @@
     picked = lax.dot_general(picks, rest, (((0,), (0,)), ((), ())), preferred_element_type=jnp.float32)
     weight = jnp.transpose(jnp.broadcast_to(gates[...], (LANES, n_tok)))
     weight = jnp.concatenate([weight] * parts, axis=1)
-    mixed[...] = (tokens[...].astype(jnp.float32) + weight * picked).astype(jnp.bfloat16)
+    gated[...] = weight * picked
     left = 2 * N // ROWS - 1
     for box, sem in ((outbox, out_sem), (results, back_sem)):
         pltpu.make_async_copy(box.at[pl.ds(0, left)], box.at[pl.ds(0, left)], sem).wait()
@@ -190,11 +193,11 @@
     n_tok, width = tokens.shape
     hidden = w_in.shape[2]
     box = pltpu.VMEM((2 * N // ROWS, width // LANES, ROWS, LANES), jnp.bfloat16)
-    vmem, anywhere = pl.BlockSpec(memory_space=pltpu.VMEM), pl.BlockSpec(memory_space=pl.ANY)
-    return pl.pallas_call(
+    vmem, hbm = pl.BlockSpec(memory_space=pltpu.VMEM), pl.BlockSpec(memory_space=pltpu.HBM)
+    gated = pl.pallas_call(
         kernel,
-        out_shape=jax.ShapeDtypeStruct(tokens.shape, tokens.dtype),
-        in_specs=[anywhere] * 7,
+        out_shape=jax.ShapeDtypeStruct(tokens.shape, jnp.float32),
+        in_specs=[hbm] * 7,
         out_specs=vmem,
         scratch_shapes=[
             pltpu.VMEM((n_tok, width), tokens.dtype),
@@ -206,7 +209,7 @@
             pltpu.VMEM((width, hidden), jnp.bfloat16),
             pltpu.VMEM((width, hidden), jnp.bfloat16),
             pltpu.VMEM((PARTNERS * 2, hidden), jnp.bfloat16),
-            pltpu.SemaphoreType.REGULAR,
+            pltpu.SemaphoreType.REGULAR((NZ,)),
             pltpu.SemaphoreType.DMA((5,)),
             pltpu.SemaphoreType.DMA((2,)),
             pltpu.SemaphoreType.DMA,
@@ -214,9 +217,10 @@
             pltpu.SemaphoreType.DMA,
             pltpu.SemaphoreType.DMA,
         ],
-        compiler_params=pltpu.CompilerParams(collective_id=0, has_side_effects=True),
-    )(tokens, norm_gain, gates.reshape(1, n_tok), expert_ids.reshape(1, n_tok),
-      slots.reshape(1, n_tok), w_in, w_out)
+        compiler_params=pltpu.CompilerParams(collective_id=0, has_side_effects=True, vmem_limit_bytes=VMEM_LIMIT),
+    )(*[pltpu.with_memory_space_constraint(v, pltpu.HBM) for v in (tokens, norm_gain, gates.reshape(1, n_tok), expert_ids.reshape(1, n_tok),
+      slots.reshape(1, n_tok), w_in, w_out)])
+    return (tokens.astype(jnp.float32) + gated).astype(tokens.dtype)
 
 
 def solution(mesh):

time: 58.5 us -> 55.8 us (0.954)
  local copies, waits for them, and re-layouts: 1.77 us -> 0.01 us
  Pallas kernels: 56.6 us -> 54.9 us
  other arithmetic: 0 us -> 0.82 us
    unnamed x1 -> x2, local copies, waits for them, and re-layouts: 1.77 us -> 0.01 us
    pallas_call x1, Pallas kernels: 56.6 us -> 54.9 us  [local(): pl.pallas_call(kernel, out_shape=jax.ShapeDtypeStruct(tokens.shape, jnp.f...]
    convert_element_type x0 -> x1, other arithmetic: none -> 0.82 us  [local(): return (tokens.astype(jnp.float32) + gated).astype(tokens.dtype)]
where the time goes in v4:
time: 55.8 us; the launch traced here: 55.7 us
  Pallas kernels  54.9 us (98%)
  other arithmetic  0.82 us (1%)
    pallas_call x1, Pallas kernels, local(): pl.pallas_call(kernel, out_shape=jax.ShapeDtypeStruct(tokens.shape, jnp.f...  54.9 us

profile of v4, /device:TPU:1, one launch (start us, length us, event | category | flops | bytes accessed | tf_op | source)
XLA Modules:
  0.0 55.7 jit_solution(13823777004449026104)
XLA Ops:
  0.0 0.0 copy-start
  0.0 54.9 %shard_map.73 = f32[256,768]{1,0:T(8,128)S(1)} custom-call(bf16[256,768]{1,0:T(8,128)(2,1)} %tokens_hbm.1, f32[768]{0:T(1024)} %gain_hbm.1, f32[1,256]{1,0:T(1,128)} %bitcast.3, s32[1,256]{1,0:T(1,128)} %bitcast.4, s32[1,256]{1,0:T(1,128)} %bitcast.5, bf16[1,768,3072]{2,1,0:T(8,128)(2,1)} %w_in.1, bf16[1,768,3072]{2,1,0:T(8,128)(2,1)} %w_out.1), custom_call_target="tpu_custom_call" | custom-call | tf_op jit(solution)/shard_map/pallas_call | solution.py:197
  54.9 0.0 copy-done
  54.9 0.8 %add_convert_fusion = bf16[256,768]{1,0:T(8,128)(2,1)} fusion(f32[256,768]{1,0:T(8,128)S(1)} %shard_map.73, bf16[256,768]{1,0:T(8,128)(2,1)S(1)} %copy-done), kind=kLoop, calls=%fused_computation | loop fusion | flops 589824 | bytes 1572864 | tf_op jit(solution)/shard_map/convert_element_type | solution.py:223
Async XLA Ops:
  0.0 54.9 %copy-start = (bf16[256,768]{1,0:T(8,128)(2,1)S(1)}, bf16[256,768]{1,0:T(8,128)(2,1)}, u32[]{:S(2)}) copy-start(bf16[256,768]{1,0:T(8,128)(2,1)} %tokens_hbm.1) | copy-start | bytes 1179652

commit v5 on v4

--- a/solution.py
+++ b/solution.py
@@ -12,12 +12,14 @@
 N = NX * NY * NZ * NC
 LANES, ROWS = 128, 16
 VMEM_LIMIT = 24 * 1024 * 1024
-CHUNKS = ((0, 2), (1, 2))
-PARTNERS = N // len(CHUNKS)
-ALONG_Z = NZ // len(CHUNKS)
-TILES = PARTNERS * 2 // ROWS
-GROUPS = ((0, (1, 3)), (0, (2,)), (1, (0, 3)), (1, (1, 2)))
+CHUNKS = ((0, 3, 5), (4, 1, 7), (2, 6))
+PLANE_TILES = NX * NY * NC * 2 // ROWS
+GROUPS = ((0, (1,)), (0, (2,)), (1, (1,)), (1, (2,)), (1, (0,)), (2, (0,)), (2, (1,)))
 PLANE = [(dc, dx) for dc in range(NC) for dx in range(NX)]
+
+
+def first_tile(chunk):
+    return sum(map(len, CHUNKS[:chunk])) * PLANE_TILES
 
 
 class Place:
@@ -98,11 +100,10 @@
     here = place.row(0)
 
     def post(chunk, dy, row, combos):
-        first, step = CHUNKS[chunk]
         for a, dc, dx in combos:
-            number, tile, i = place.at(row, dx, first + step * a, dc)
+            number, tile, i = place.at(row, dx, CHUNKS[chunk][a], dc)
             pltpu.make_async_remote_copy(
-                pair(outbox, tile, i), pair(inbox, chunk * TILES + dy * ALONG_Z + a, dc * NX + dx),
+                pair(outbox, tile, i), pair(inbox, first_tile(chunk) + dy * len(CHUNKS[chunk]) + a, dc * NX + dx),
                 out_sem, in_sem.at[chunk], device_id=number, device_id_type=LOGICAL,
             ).start()
 
@@ -110,7 +111,7 @@
     for dz in range(1, NZ):
         pl.semaphore_signal(met.at[NZ - dz], inc=1, device_id=place.at(here, 0, dz, 0)[0], device_id_type=LOGICAL)
     for chunk in range(len(CHUNKS)):
-        post(chunk, 0, here, [(a, 0, 0) for a in range(1 if chunk == 0 else 0, ALONG_Z)])
+        post(chunk, 0, here, [(a, 0, 0) for a in range(1 if chunk == 0 else 0, len(CHUNKS[chunk]))])
     post(0, 0, here, [(0, dc, dx) for dc, dx in PLANE if dc or dx])
 
     def post_row(dy, _):
@@ -121,9 +122,8 @@
     own = pltpu.make_async_copy(pair(outbox, me // 8, lax.rem(me, 8)), pair(inbox, 0, 0), in_sem.at[0])
     own.start()
     for chunk, group in GROUPS:
-        first, step = CHUNKS[chunk]
         for a in group:
-            pl.semaphore_wait(met.at[first + step * a], 1)
+            pl.semaphore_wait(met.at[CHUNKS[chunk][a]], 1)
         post(chunk, 0, here, [(a, dc, dx) for dc, dx in PLANE for a in group if dc or dx])
 
         def post_rest(dy, _):
@@ -136,43 +136,46 @@
 
     near = place.at(here, 0, 0, 1)[0]
     for chunk in range(len(CHUNKS)):
-        tiles = pl.ds(chunk * TILES, TILES)
+        count = len(CHUNKS[chunk]) * PLANE_TILES
+        tiles = pl.ds(first_tile(chunk), count)
+        at_rows = pl.ds(0, count * ROWS)
         pltpu.make_async_remote_copy(
             inbox.at[tiles], inbox.at[tiles], out_sem, in_sem.at[chunk], device_id=near, device_id_type=LOGICAL
         ).wait_recv()
-        rows = columns(inbox, tiles, TILES)
+        rows = columns(inbox, tiles, count)
 
         def widen(k, _):
             at = pl.ds(pl.multiple_of(k * 256, 256), 256)
             h = jnp.dot(rows, w1[:, at], preferred_element_type=jnp.float32)
-            hidden[:, at] = jnp.maximum(h, 0.0).astype(jnp.bfloat16)
+            hidden[at_rows, at] = jnp.maximum(h, 0.0).astype(jnp.bfloat16)
             return 0
 
         lax.fori_loop(0, w1.shape[1] // 256, widen, 0)
         for j in range(parts // 2):
             r = lax.dot_general(
-                hidden[...], w2[j * 256 : j * 256 + 256, :], (((1,), (1,)), ((), ())), preferred_element_type=jnp.float32
+                hidden[at_rows, :], w2[j * 256 : j * 256 + 256, :], (((1,), (1,)), ((), ())), preferred_element_type=jnp.float32
             ).astype(jnp.bfloat16)
             for half in range(2):
-                results[tiles, 2 * j + half] = r[:, half * LANES : (half + 1) * LANES].reshape(TILES, ROWS, LANES)
+                results[tiles, 2 * j + half] = r[:, half * LANES : (half + 1) * LANES].reshape(count, ROWS, LANES)
 
         home = pair(returned, me // 8, lax.rem(me, 8))
 
         def reply(dy, row, combos):
-            first, step = CHUNKS[chunk]
             for a, dc, dx in combos:
-                number = place.at(row, -dx % NX, -(first + step * a) % NZ, dc)[0]
+                number = place.at(row, -dx % NX, -CHUNKS[chunk][a] % NZ, dc)[0]
                 pltpu.make_async_remote_copy(
-                    pair(results, chunk * TILES + dy * ALONG_Z + a, dc * NX + dx), home,
+                    pair(results, first_tile(chunk) + dy * len(CHUNKS[chunk]) + a, dc * NX + dx), home,
                     back_sem, home_sem, device_id=number, device_id_type=LOGICAL,
                 ).start()
 
-        def reply_row(dy, _):
-            reply(dy, place.row(NY - dy), [(a, dc, dx) for dc, dx in PLANE for a in range(ALONG_Z)])
-            return 0
-
-        reply(0, here, [(a, dc, dx) for dc, dx in PLANE for a in range(ALONG_Z) if chunk or a or dc or dx])
-        lax.fori_loop(1, NY, reply_row, 0)
+        for a in range(len(CHUNKS[chunk])):
+            reply(0, here, [(a, dc, dx) for dc, dx in PLANE if CHUNKS[chunk][a] or dc or dx])
+
+            def reply_row(dy, _):
+                reply(dy, place.row(NY - dy), [(a, dc, dx) for dc, dx in PLANE])
+                return 0
+
+            lax.fori_loop(1, NY, reply_row, 0)
         if chunk == 0:
             pltpu.make_async_copy(pair(results, 0, 0), home, home_sem).start()
 
@@ -208,7 +211,7 @@
             box, box, box, box,
             pltpu.VMEM((width, hidden), jnp.bfloat16),
             pltpu.VMEM((width, hidden), jnp.bfloat16),
-            pltpu.VMEM((PARTNERS * 2, hidden), jnp.bfloat16),
+            pltpu.VMEM((max(map(len, CHUNKS)) * PLANE_TILES * ROWS, hidden), jnp.bfloat16),
             pltpu.SemaphoreType.REGULAR((NZ,)),
             pltpu.SemaphoreType.DMA((5,)),
             pltpu.SemaphoreType.DMA((2,)),

time: 55.8 us -> 53.2 us (0.953)
  Pallas kernels: 54.9 us -> 51.8 us
    pallas_call x1, Pallas kernels: 54.9 us -> 51.8 us  [local(): pl.pallas_call(kernel, out_shape=jax.ShapeDtypeStruct(tokens.shape, jnp.f...]
where the time goes in v5:
time: 53.2 us; the launch traced here: 52.6 us
  Pallas kernels  51.8 us (97%)
  other arithmetic  0.82 us (2%)
    pallas_call x1, Pallas kernels, local(): pl.pallas_call(kernel, out_shape=jax.ShapeDtypeStruct(tokens.shape, jnp.f...  51.8 us

profile of v5, /device:TPU:1, one launch (start us, length us, event | category | flops | bytes accessed | tf_op | source)
XLA Modules:
  0.0 52.6 jit_solution(1926502508060842289)
XLA Ops:
  0.0 0.0 copy-start
  0.0 51.8 %shard_map.73 = f32[256,768]{1,0:T(8,128)S(1)} custom-call(bf16[256,768]{1,0:T(8,128)(2,1)} %tokens_hbm.1, f32[768]{0:T(1024)} %gain_hbm.1, f32[1,256]{1,0:T(1,128)} %bitcast.3, s32[1,256]{1,0:T(1,128)} %bitcast.4, s32[1,256]{1,0:T(1,128)} %bitcast.5, bf16[1,768,3072]{2,1,0:T(8,128)(2,1)} %w_in.1, bf16[1,768,3072]{2,1,0:T(8,128)(2,1)} %w_out.1), custom_call_target="tpu_custom_call" | custom-call | tf_op jit(solution)/shard_map/pallas_call | solution.py:200
  51.8 0.0 copy-done
  51.8 0.8 %add_convert_fusion = bf16[256,768]{1,0:T(8,128)(2,1)} fusion(f32[256,768]{1,0:T(8,128)S(1)} %shard_map.73, bf16[256,768]{1,0:T(8,128)(2,1)S(1)} %copy-done), kind=kLoop, calls=%fused_computation | loop fusion | flops 589824 | bytes 1572864 | tf_op jit(solution)/shard_map/convert_element_type | solution.py:226
Async XLA Ops:
  0.0 51.8 %copy-start = (bf16[256,768]{1,0:T(8,128)(2,1)S(1)}, bf16[256,768]{1,0:T(8,128)(2,1)}, u32[]{:S(2)}) copy-start(bf16[256,768]{1,0:T(8,128)(2,1)} %tokens_hbm.1) | copy-start | bytes 1179652

commit v6 on v5

--- a/solution.py
+++ b/solution.py
@@ -145,12 +145,12 @@
         rows = columns(inbox, tiles, count)
 
         def widen(k, _):
-            at = pl.ds(pl.multiple_of(k * 256, 256), 256)
+            at = pl.ds(pl.multiple_of(k * 512, 512), 512)
             h = jnp.dot(rows, w1[:, at], preferred_element_type=jnp.float32)
             hidden[at_rows, at] = jnp.maximum(h, 0.0).astype(jnp.bfloat16)
             return 0
 
-        lax.fori_loop(0, w1.shape[1] // 256, widen, 0)
+        lax.fori_loop(0, w1.shape[1] // 512, widen, 0)
         for j in range(parts // 2):
             r = lax.dot_general(
                 hidden[at_rows, :], w2[j * 256 : j * 256 + 256, :], (((1,), (1,)), ((), ())), preferred_element_type=jnp.float32

time: 53.2 us -> 52.2 us (0.981)
  Pallas kernels: 51.8 us -> 50.8 us
    pallas_call x1, Pallas kernels: 51.8 us -> 50.8 us  [local(): pl.pallas_call(kernel, out_shape=jax.ShapeDtypeStruct(tokens.shape, jnp.f...]
where the time goes in v6:
time: 52.2 us; the launch traced here: 51.6 us
  Pallas kernels  50.8 us (97%)
  other arithmetic  0.82 us (2%)
    pallas_call x1, Pallas kernels, local(): pl.pallas_call(kernel, out_shape=jax.ShapeDtypeStruct(tokens.shape, jnp.f...  50.8 us

profile of v6, /device:TPU:1, one launch (start us, length us, event | category | flops | bytes accessed | tf_op | source)
XLA Modules:
  0.0 51.6 jit_solution(7418143872532596648)
XLA Ops:
  0.0 0.0 copy-start
  0.0 50.8 %shard_map.73 = f32[256,768]{1,0:T(8,128)S(1)} custom-call(bf16[256,768]{1,0:T(8,128)(2,1)} %tokens_hbm.1, f32[768]{0:T(1024)} %gain_hbm.1, f32[1,256]{1,0:T(1,128)} %bitcast.3, s32[1,256]{1,0:T(1,128)} %bitcast.4, s32[1,256]{1,0:T(1,128)} %bitcast.5, bf16[1,768,3072]{2,1,0:T(8,128)(2,1)} %w_in.1, bf16[1,768,3072]{2,1,0:T(8,128)(2,1)} %w_out.1), custom_call_target="tpu_custom_call" | custom-call | tf_op jit(solution)/shard_map/pallas_call | solution.py:200
  50.8 0.0 copy-done
  50.8 0.8 %add_convert_fusion = bf16[256,768]{1,0:T(8,128)(2,1)} fusion(f32[256,768]{1,0:T(8,128)S(1)} %shard_map.73, bf16[256,768]{1,0:T(8,128)(2,1)S(1)} %copy-done), kind=kLoop, calls=%fused_computation | loop fusion | flops 589824 | bytes 1572864 | tf_op jit(solution)/shard_map/convert_element_type | solution.py:226
Async XLA Ops:
  0.0 50.8 %copy-start = (bf16[256,768]{1,0:T(8,128)(2,1)S(1)}, bf16[256,768]{1,0:T(8,128)(2,1)}, u32[]{:S(2)}) copy-start(bf16[256,768]{1,0:T(8,128)(2,1)} %tokens_hbm.1) | copy-start | bytes 1179652

commit v7 on v6

--- a/solution.py
+++ b/solution.py
@@ -52,7 +52,7 @@
 def greet(place):
     barrier = pltpu.get_barrier_semaphore()
     rows = [place.row(dy) for dy in range(NY)]
-    for dz in range(1, NZ):
+    for dz in (4, 3, 5, 2, 6, 1, 7):
         pl.semaphore_signal(barrier, inc=1, device_id=place.at(rows[0], 0, dz, 0)[0], device_id_type=LOGICAL)
     for dy in range(NY):
         for dc, dx in PLANE:
@@ -108,7 +108,7 @@
             ).start()
 
     pl.semaphore_wait(pltpu.get_barrier_semaphore(), NX * NY * NC + NZ - 2)
-    for dz in range(1, NZ):
+    for dz in (5, 3, 7, 1, 4, 6, 2):
         pl.semaphore_signal(met.at[NZ - dz], inc=1, device_id=place.at(here, 0, dz, 0)[0], device_id_type=LOGICAL)
     for chunk in range(len(CHUNKS)):
         post(chunk, 0, here, [(a, 0, 0) for a in range(1 if chunk == 0 else 0, len(CHUNKS[chunk]))])

time: 52.2 us -> 52.2 us (level)
  no operation moved by 1% of the time
where the time goes in v7:
time: 52.2 us; the launch traced here: 51.6 us
  Pallas kernels  50.8 us (97%)
  other arithmetic  0.82 us (2%)
    pallas_call x1, Pallas kernels, local(): pl.pallas_call(kernel, out_shape=jax.ShapeDtypeStruct(tokens.shape, jnp.f...  50.8 us

profile of v7, /device:TPU:1, one launch (start us, length us, event | category | flops | bytes accessed | tf_op | source)
XLA Modules:
  0.0 51.6 jit_solution(13068470197550417826)
XLA Ops:
  0.0 0.0 copy-start
  0.0 50.8 %shard_map.73 = f32[256,768]{1,0:T(8,128)S(1)} custom-call(bf16[256,768]{1,0:T(8,128)(2,1)} %tokens_hbm.1, f32[768]{0:T(1024)} %gain_hbm.1, f32[1,256]{1,0:T(1,128)} %bitcast.3, s32[1,256]{1,0:T(1,128)} %bitcast.4, s32[1,256]{1,0:T(1,128)} %bitcast.5, bf16[1,768,3072]{2,1,0:T(8,128)(2,1)} %w_in.1, bf16[1,768,3072]{2,1,0:T(8,128)(2,1)} %w_out.1), custom_call_target="tpu_custom_call" | custom-call | tf_op jit(solution)/shard_map/pallas_call | solution.py:200
  50.8 0.0 copy-done
  50.8 0.8 %add_convert_fusion = bf16[256,768]{1,0:T(8,128)(2,1)} fusion(f32[256,768]{1,0:T(8,128)S(1)} %shard_map.73, bf16[256,768]{1,0:T(8,128)(2,1)S(1)} %copy-done), kind=kLoop, calls=%fused_computation | loop fusion | flops 589824 | bytes 1572864 | tf_op jit(solution)/shard_map/convert_element_type | solution.py:226
Async XLA Ops:
  0.0 50.8 %copy-start = (bf16[256,768]{1,0:T(8,128)(2,1)S(1)}, bf16[256,768]{1,0:T(8,128)(2,1)}, u32[]{:S(2)}) copy-start(bf16[256,768]{1,0:T(8,128)(2,1)} %tokens_hbm.1) | copy-start | bytes 1179652

commit v8 on v6

--- a/solution.py
+++ b/solution.py
@@ -151,12 +151,12 @@
             return 0
 
         lax.fori_loop(0, w1.shape[1] // 512, widen, 0)
-        for j in range(parts // 2):
+        for j in range(0, parts, 6):
             r = lax.dot_general(
-                hidden[at_rows, :], w2[j * 256 : j * 256 + 256, :], (((1,), (1,)), ((), ())), preferred_element_type=jnp.float32
+                hidden[at_rows, :], w2[j * LANES : (j + 6) * LANES, :], (((1,), (1,)), ((), ())), preferred_element_type=jnp.float32
             ).astype(jnp.bfloat16)
-            for half in range(2):
-                results[tiles, 2 * j + half] = r[:, half * LANES : (half + 1) * LANES].reshape(count, ROWS, LANES)
+            for part in range(6):
+                results[tiles, j + part] = r[:, part * LANES : (part + 1) * LANES].reshape(count, ROWS, LANES)
 
         home = pair(returned, me // 8, lax.rem(me, 8))
 

time: 52.2 us -> 52.1 us (level)
  no operation moved by 1% of the time
where the time goes in v8:
time: 52.1 us; the launch traced here: 51.6 us
  Pallas kernels  50.8 us (98%)
  other arithmetic  0.82 us (2%)
    pallas_call x1, Pallas kernels, local(): pl.pallas_call(kernel, out_shape=jax.ShapeDtypeStruct(tokens.shape, jnp.f...  50.8 us

profile of v8, /device:TPU:1, one launch (start us, length us, event | category | flops | bytes accessed | tf_op | source)
XLA Modules:
  0.0 51.6 jit_solution(16639705228576560536)
XLA Ops:
  0.0 0.0 copy-start
  0.0 50.8 %shard_map.73 = f32[256,768]{1,0:T(8,128)S(1)} custom-call(bf16[256,768]{1,0:T(8,128)(2,1)} %tokens_hbm.1, f32[768]{0:T(1024)} %gain_hbm.1, f32[1,256]{1,0:T(1,128)} %bitcast.3, s32[1,256]{1,0:T(1,128)} %bitcast.4, s32[1,256]{1,0:T(1,128)} %bitcast.5, bf16[1,768,3072]{2,1,0:T(8,128)(2,1)} %w_in.1, bf16[1,768,3072]{2,1,0:T(8,128)(2,1)} %w_out.1), custom_call_target="tpu_custom_call" | custom-call | tf_op jit(solution)/shard_map/pallas_call | solution.py:200
  50.8 0.0 copy-done
  50.8 0.8 %add_convert_fusion = bf16[256,768]{1,0:T(8,128)(2,1)} fusion(f32[256,768]{1,0:T(8,128)S(1)} %shard_map.73, bf16[256,768]{1,0:T(8,128)(2,1)S(1)} %copy-done), kind=kLoop, calls=%fused_computation | loop fusion | flops 589824 | bytes 1572864 | tf_op jit(solution)/shard_map/convert_element_type | solution.py:226
Async XLA Ops:
  0.0 50.8 %copy-start = (bf16[256,768]{1,0:T(8,128)(2,1)S(1)}, bf16[256,768]{1,0:T(8,128)(2,1)}, u32[]{:S(2)}) copy-start(bf16[256,768]{1,0:T(8,128)(2,1)} %tokens_hbm.1) | copy-start | bytes 1179652
